TPU v7x, 32 devices: a whole 2x2x4 slice. The times are simulated.
32 devices in a mesh: layer: 2 (over x), blk: 16 (over z, y, core).
Axes of the slice: x: 2, y: 2, z: 4, core: 2. Of those that a mesh axis runs over, the one named last changes fastest.
Arguments:
- points: bfloat16 [12288, 256], P('blk'), may hold values from -8.4 to 8.4
- labels: int32 [12288], P('blk'), may hold values from 0 to 255, as said below
Outputs:
- distance: float32 [12288, 256], P('blk')
Inputs may be any that keep to these rules, and one draw needn't show every extreme that they name: `labels`: every cluster is named by at least one point.
All inputs are finite; a program needn't handle non-finite values.
Results may differ from a plain program's by a relative error of at most 0.00034.
Values may be sent and summed in bfloat16 or wider, within the bound.
A program may use at most 64 MiB of HBM per device.

v0:
```python
import jax
import jax.numpy as jnp
from jax import lax
from jax.sharding import PartitionSpec as P

K = 256


def as_sent(x):
    return jax.tree.map(lambda a: a.astype(jnp.bfloat16) if a.dtype == jnp.float32 else a, x)


def from_behind(x, axis, by):
    devices = lax.axis_size(axis)
    return lax.ppermute(x, axis, [(i, (i + by) % devices) for i in range(devices)])


def choose_where(chosen, shifted, carried):
    return tuple(
        (jnp.where(chosen, new_part, old_part) for new_part, old_part in zip(shifted, carried))
    )


def shards(points, labels):
    feature_width = points.shape[1]
    own_rows = points.shape[0]
    layers = lax.axis_size("layer")
    blocks = lax.axis_size("blk")
    visit_count = blocks // layers
    half_steps = visit_count // 2
    layer_idx = lax.axis_index("layer")
    offset_bits = (layers - 1).bit_length()
    own_sq = jnp.sum(jnp.square(points.astype(jnp.float32)), axis=1)
    cluster_ids = jnp.arange(K, dtype=jnp.float32)
    tagged = labels.astype(jnp.bfloat16)

    def accumulate(partial_value, visiting, block_tags):
        visit_sq = jnp.sum(jnp.square(visiting.astype(jnp.float32)), axis=1)
        gram_block = lax.dot_general(
            points, visiting, (((1,), (1,)), ((), ())), preferred_element_type=jnp.float32
        )
        kernel = jnp.exp(
            -(own_sq[:, None] + visit_sq[None, :] - 2.0 * gram_block) / feature_width
        ).astype(jnp.bfloat16)
        onehot = (block_tags.astype(jnp.float32)[:, None] == cluster_ids[None, :]).astype(
            jnp.bfloat16
        )
        return partial_value + jnp.dot(kernel, onehot, preferred_element_type=jnp.float32)

    initial = jnp.zeros((own_rows, K), jnp.float32)
    carried = (points, tagged)
    for bit_pos in range(offset_bits):
        shifted = jax.tree.map(
            lambda part, own: part.astype(own.dtype),
            from_behind(as_sent(carried), "blk", visit_count << bit_pos),
            carried,
        )
        carried = choose_where(layer_idx >> bit_pos & 1 == 1, shifted, carried)
    climbing = jax.tree.map(
        lambda part, own: part.astype(own.dtype),
        from_behind(as_sent(carried), "blk", half_steps),
        carried,
    )
    falling = jax.tree.map(
        lambda part, own: part.astype(own.dtype),
        from_behind(as_sent(carried), "blk", half_steps - 1),
        carried,
    )
    partial_value = accumulate(
        accumulate(initial, climbing[0], climbing[1]), falling[0], falling[1]
    )

    def split_turn(turn_index, loop_state):
        partial_now, climb_pts, climb_tags, fall_pts, fall_tags = loop_state
        climb_pts, climb_tags = from_behind((climb_pts, climb_tags), "blk", 1)
        fall_pts, fall_tags = from_behind((fall_pts, fall_tags), "blk", -1)
        partial_now = accumulate(partial_now, climb_pts, climb_tags)
        partial_now = accumulate(partial_now, fall_pts, fall_tags)
        return (partial_now, climb_pts, climb_tags, fall_pts, fall_tags)

    partial_value = lax.fori_loop(
        0,
        half_steps - 1,
        split_turn,
        (partial_value, climbing[0], climbing[1], falling[0], falling[1]),
    )[0]
    row_sums = lax.psum(partial_value, "layer")
    member_f = (labels[:, None] == jnp.arange(K, dtype=jnp.int32)[None, :]).astype(jnp.float32)
    within, counts = lax.psum(
        (jnp.sum(member_f * row_sums, axis=0), jnp.sum(member_f, axis=0)), "blk"
    )
    distance = 1.0 - 2.0 * row_sums / counts[None, :] + within[None, :] / (counts * counts)[None, :]
    return distance


def solution(mesh):
    in_specs = (P("blk", None), P("blk"))
    out_specs = P("blk", None)
    return jax.shard_map(shards, mesh=mesh, in_specs=in_specs, out_specs=out_specs, check_vma=False)
```

profile of v0, /device:TPU:0, one launch (start us, length us, event | category | flops | bytes accessed | tf_op | source)
XLA Modules:
  0.0 178.2 jit_solution(9994201577379634457)
XLA Ops:
  6.5 4.1 %collective-permute-start.4 = (bf16[768,256]{1,0:T(8,128)(2,1)}, bf16[768,256]{1,0:T(8,128)(2,1)S(1)}, u32[]{:S(2)}, u32[]{:S(2)}) collective-permute-start(bf16[768,256]{1,0:T(8,128)(2,1)} %param.4), channel_id=1, source_target_pairs={{0,8},{1,9},{2,10},{3,11},{4,12},{5,13},{6,14},{7,15},{8,0},{9,1},... | collective-permute-start | bytes 1179656 | tf_op jit(solution)/shard_map/ppermute | solution.py:15
  10.6 17.8 %collective-permute-done.4 = bf16[768,256]{1,0:T(8,128)(2,1)S(1)} collective-permute-done((bf16[768,256]{1,0:T(8,128)(2,1)}, bf16[768,256]{1,0:T(8,128)(2,1)S(1)}, u32[]{:S(2)}, u32[]{:S(2)}) %collective-permute-start.4) | collective-permute-done | bytes 393248 | tf_op jit(solution)/shard_map/ppermute | solution.py:15
  28.4 1.0 broadcast_select_fusion
  29.7 5.0 %collective-permute-start.5 = (bf16[768,256]{1,0:T(8,128)(2,1)S(1)}, bf16[768,256]{1,0:T(8,128)(2,1)S(1)}, u32[]{:S(2)}, u32[]{:S(2)}) collective-permute-start(bf16[768,256]{1,0:T(8,128)(2,1)S(1)} %broadcast_select_fusion), channel_id=1, source_target_pairs={{0,4},{1,5},{2,6},{3,7},{4,8},{5,9},{6,10},{7,11},{8,12},{9,13},{1... | collective-permute-start | bytes 1179656 | tf_op jit(solution)/shard_map/ppermute | solution.py:15
  34.7 5.6 %collective-permute-start.9 = (bf16[768]{0:T(1024)(128)(2,1)S(1)}, bf16[768]{0:T(1024)(128)(2,1)S(1)}, u32[]{:S(2)}, u32[]{:S(2)}) collective-permute-start(bf16[768]{0:T(1024)(128)(2,1)S(1)} %broadcast_select_fusion.1), channel_id=1, source_target_pairs={{0,3},{1,4},{2,5},{3,6},{4,7},{5,8},{6,9},{7,10},{8,11},{9,12},{10... | collective-permute-start | bytes 4616 | tf_op jit(solution)/shard_map/ppermute | solution.py:15
  40.4 3.7 %collective-permute-start.7 = (bf16[768]{0:T(1024)(128)(2,1)S(1)}, bf16[768]{0:T(1024)(128)(2,1)S(1)}, u32[]{:S(2)}, u32[]{:S(2)}) collective-permute-start(bf16[768]{0:T(1024)(128)(2,1)S(1)} %broadcast_select_fusion.1), channel_id=1, source_target_pairs={{0,4},{1,5},{2,6},{3,7},{4,8},{5,9},{6,10},{7,11},{8,12},{9,13},{1... | collective-permute-start | bytes 4616 | tf_op jit(solution)/shard_map/ppermute | solution.py:15
  44.3 2.8 %collective-permute-done.9 = bf16[768]{0:T(1024)(128)(2,1)S(1)} collective-permute-done((bf16[768]{0:T(1024)(128)(2,1)S(1)}, bf16[768]{0:T(1024)(128)(2,1)S(1)}, u32[]{:S(2)}, u32[]{:S(2)}) %collective-permute-start.9) | collective-permute-done | bytes 1568 | tf_op jit(solution)/shard_map/ppermute | solution.py:15
  47.5 0.9 fusion.29
  48.4 0.9 fusion.30
  49.3 50.8 %while.20 = (s32[]{:T(128)}, f32[768,256]{1,0:T(8,128)S(1)}, bf16[768,256]{1,0:T(8,128)(2,1)S(1)}, bf16[768]{0:T(1024)(128)(2,1)S(1)}, bf16[768,256]{1,0:T(8,128...) while((s32[]{:T(128)}, f32[768,256]{1,0:T(8,128)S(1)}, ...), condition=%wide.region_6.7_spmd.clone.clone, body=%wide.region_3.6_spmd.clone.clone.sunk | while | flops 1217003520 | bytes 10276093 | solution.py:81
  49.4 6.5 %collective-permute-start = (bf16[768,256]{1,0:T(8,128)(2,1)S(1)}, bf16[768,256]{1,0:T(8,128)(2,1)S(1)}, u32[]{:S(2)}, u32[]{:S(2)}) collective-permute-start(bf16[768,256]{1,0:T(8,128)(2,1)S(1)} %get-tuple-element.178), channel_id=1, source_target_pairs={{0,15},{1,0},{2,1},{3,2},{4,3},{5,4},{6,5},{7,6},{8,7},{9,8},{10,9... | collective-permute-start | bytes 1179656 | tf_op jit(solution)/shard_map/while/body/eval_jaxpr/ppermute | solution.py:15
  55.8 4.4 %collective-permute-start.1 = (bf16[768]{0:T(1024)(128)(2,1)S(1)}, bf16[768]{0:T(1024)(128)(2,1)S(1)}, u32[]{:S(2)}, u32[]{:S(2)}) collective-permute-start(bf16[768]{0:T(1024)(128)(2,1)S(1)} %get-tuple-element.179), channel_id=1, source_target_pairs={{0,15},{1,0},{2,1},{3,2},{4,3},{5,4},{6,5},{7,6},{8,7},{9,8},{10,9... | collective-permute-start | bytes 4616 | tf_op jit(solution)/shard_map/while/body/eval_jaxpr/ppermute | solution.py:15
  60.3 1.3 collective-permute-done.1
  61.6 4.4 %collective-permute-done.3 = bf16[768]{0:T(1024)(128)(2,1)S(1)} collective-permute-done((bf16[768]{0:T(1024)(128)(2,1)S(1)}, bf16[768]{0:T(1024)(128)(2,1)S(1)}, u32[]{:S(2)}, u32[]{:S(2)}) %collective-permute-start.3) | collective-permute-done | bytes 1568 | tf_op jit(solution)/shard_map/while/body/eval_jaxpr/ppermute | solution.py:15
  66.5 1.8 %fusion.63 = f32[768,256]{1,0:T(8,128)} fusion(bf16[768,256]{1,0:T(8,128)(2,1)S(1)} %get-tuple-element.190, bf16[768,256]{1,0:T(8,128)(2,1)S(1)} %collective-permute-done, f32[768]{0:T(1024)S(1)} %multiply_reduce_fusion.7, f32[768]{0:T(1024)S(1)} %get-tuple-element.189, f32[768]{0:T(1024)S(1)} %convert_element_type.105), kind=kOutput, calls=%fused_computation.4.clone.1 | convolution fusion | flops 607715328 | bytes 1582080 | tf_op jit(solution)/shard_map/while/body/eval_jaxpr/dot_general | solution.py:48
  68.3 2.2 %fusion.64 = f32[768,256]{1,0:T(8,128)S(1)} fusion(f32[768,256]{1,0:T(8,128)} %fusion.63, f32[768,256]{1,0:T(8,128)S(1)} %get-tuple-element.175, bf16[768,256]{1,0:T(8,128)(2,1)S(1)} %get-tuple-element.190, bf16[768,256]{1,0:T(8,128)(2,1)S(1)} %collective-permute-done.2, f32[768]{0:T(1024)S(1)} %multiply_reduce_fusion.8, ...), kind=kOutput, calls=%fused_computation.6.clone.1 | convolution fusion | flops 608108544 | bytes 3154944 | tf_op jit(solution)/shard_map/while/body/eval_jaxpr/dot_general | solution.py:48
  71.1 4.0 %collective-permute-start.1 = (bf16[768]{0:T(1024)(128)(2,1)S(1)}, bf16[768]{0:T(1024)(128)(2,1)S(1)}, u32[]{:S(2)}, u32[]{:S(2)}) collective-permute-start(bf16[768]{0:T(1024)(128)(2,1)S(1)} %get-tuple-element.179), channel_id=1, source_target_pairs={{0,15},{1,0},{2,1},{3,2},{4,3},{5,4},{6,5},{7,6},{8,7},{9,8},{10,9... | collective-permute-start | bytes 4616 | tf_op jit(solution)/shard_map/while/body/eval_jaxpr/ppermute | solution.py:15
  75.1 1.3 collective-permute-done.1
  76.4 4.4 %collective-permute-done.3 = bf16[768]{0:T(1024)(128)(2,1)S(1)} collective-permute-done((bf16[768]{0:T(1024)(128)(2,1)S(1)}, bf16[768]{0:T(1024)(128)(2,1)S(1)}, u32[]{:S(2)}, u32[]{:S(2)}) %collective-permute-start.3) | collective-permute-done | bytes 1568 | tf_op jit(solution)/shard_map/while/body/eval_jaxpr/ppermute | solution.py:15
  81.3 1.8 %fusion.63 = f32[768,256]{1,0:T(8,128)} fusion(bf16[768,256]{1,0:T(8,128)(2,1)S(1)} %get-tuple-element.190, bf16[768,256]{1,0:T(8,128)(2,1)S(1)} %collective-permute-done, f32[768]{0:T(1024)S(1)} %multiply_reduce_fusion.7, f32[768]{0:T(1024)S(1)} %get-tuple-element.189, f32[768]{0:T(1024)S(1)} %convert_element_type.105), kind=kOutput, calls=%fused_computation.4.clone.1 | convolution fusion | flops 607715328 | bytes 1582080 | tf_op jit(solution)/shard_map/while/body/eval_jaxpr/dot_general | solution.py:48
  83.1 2.2 %fusion.64 = f32[768,256]{1,0:T(8,128)S(1)} fusion(f32[768,256]{1,0:T(8,128)} %fusion.63, f32[768,256]{1,0:T(8,128)S(1)} %get-tuple-element.175, bf16[768,256]{1,0:T(8,128)(2,1)S(1)} %get-tuple-element.190, bf16[768,256]{1,0:T(8,128)(2,1)S(1)} %collective-permute-done.2, f32[768]{0:T(1024)S(1)} %multiply_reduce_fusion.8, ...), kind=kOutput, calls=%fused_computation.6.clone.1 | convolution fusion | flops 608108544 | bytes 3154944 | tf_op jit(solution)/shard_map/while/body/eval_jaxpr/dot_general | solution.py:48
  85.4 1.4 collective-permute-start.2
  86.9 3.0 %collective-permute-start.1 = (bf16[768]{0:T(1024)(128)(2,1)S(1)}, bf16[768]{0:T(1024)(128)(2,1)S(1)}, u32[]{:S(2)}, u32[]{:S(2)}) collective-permute-start(bf16[768]{0:T(1024)(128)(2,1)S(1)} %get-tuple-element.179), channel_id=1, source_target_pairs={{0,15},{1,0},{2,1},{3,2},{4,3},{5,4},{6,5},{7,6},{8,7},{9,8},{10,9... | collective-permute-start | bytes 4616 | tf_op jit(solution)/shard_map/while/body/eval_jaxpr/ppermute | solution.py:15
  89.9 1.3 collective-permute-done.1
  91.2 4.4 %collective-permute-done.3 = bf16[768]{0:T(1024)(128)(2,1)S(1)} collective-permute-done((bf16[768]{0:T(1024)(128)(2,1)S(1)}, bf16[768]{0:T(1024)(128)(2,1)S(1)}, u32[]{:S(2)}, u32[]{:S(2)}) %collective-permute-start.3) | collective-permute-done | bytes 1568 | tf_op jit(solution)/shard_map/while/body/eval_jaxpr/ppermute | solution.py:15
  96.1 1.8 %fusion.63 = f32[768,256]{1,0:T(8,128)} fusion(bf16[768,256]{1,0:T(8,128)(2,1)S(1)} %get-tuple-element.190, bf16[768,256]{1,0:T(8,128)(2,1)S(1)} %collective-permute-done, f32[768]{0:T(1024)S(1)} %multiply_reduce_fusion.7, f32[768]{0:T(1024)S(1)} %get-tuple-element.189, f32[768]{0:T(1024)S(1)} %convert_element_type.105), kind=kOutput, calls=%fused_computation.4.clone.1 | convolution fusion | flops 607715328 | bytes 1582080 | tf_op jit(solution)/shard_map/while/body/eval_jaxpr/dot_general | solution.py:48
  97.9 2.2 %fusion.64 = f32[768,256]{1,0:T(8,128)S(1)} fusion(f32[768,256]{1,0:T(8,128)} %fusion.63, f32[768,256]{1,0:T(8,128)S(1)} %get-tuple-element.175, bf16[768,256]{1,0:T(8,128)(2,1)S(1)} %get-tuple-element.190, bf16[768,256]{1,0:T(8,128)(2,1)S(1)} %collective-permute-done.2, f32[768]{0:T(1024)S(1)} %multiply_reduce_fusion.8, ...), kind=kOutput, calls=%fused_computation.6.clone.1 | convolution fusion | flops 608108544 | bytes 3154944 | tf_op jit(solution)/shard_map/while/body/eval_jaxpr/dot_general | solution.py:48
  100.2 0.9 copy-done.2
  101.1 34.8 %all-reduce.3.cloned.1.call-done = f32[768,256]{1,0:T(8,128)} async-done(((f32[768,256]{1,0:T(8,128)}), f32[768,256]{1,0:T(8,128)}) %all-reduce.3.cloned.1.call-update) | async-done | bytes 786448 | tf_op jit(solution)/shard_map/psum | solution.py:87
  135.9 1.4 convert_reduce_fusion
  137.3 33.0 %all-reduce = (f32[256]{0:T(256)S(1)}, f32[256]{0:T(256)S(1)}) all-reduce(f32[256]{0:T(256)S(1)} %get-tuple-element.97, f32[256]{0:T(256)S(1)} %get-tuple-element.96), channel_id=1, replica_groups=mesh['layer'=2,'blk'=16] {'blk'}, use_global_device_ids=true, to_apply=%region_11.12 | all-reduce | flops 512 | bytes 4096 | tf_op jit(solution)/shard_map/psum | solution.py:89
  170.4 1.0 subtract_add_fusion
  (60 shorter events, 2.7 us)
Async XLA Ops:
  6.5 37.6 %copy-start.1 = (bf16[768,256]{1,0:T(8,128)(2,1)S(1)}, bf16[768,256]{1,0:T(8,128)(2,1)}, u32[]{:S(2)}) copy-start(bf16[768,256]{1,0:T(8,128)(2,1)} %param.4) | copy-start | bytes 1179652
  6.5 23.1 %copy-start.3 = (s32[768]{0:T(1024)S(1)}, s32[768]{0:T(1024)}, u32[]{:S(2)}) copy-start(s32[768]{0:T(1024)} %param.5) | copy-start | bytes 9220
  6.5 129.4 %all-reduce.3.cloned.1.call-start = ((), (), s32[]{:S(2)}) async-start(), calls=%async_computation | async-start | bytes 1572864 | tf_op jit(solution)/shard_map/psum | solution.py:87
  6.5 21.9 %collective-permute-start.4 = (bf16[768,256]{1,0:T(8,128)(2,1)}, bf16[768,256]{1,0:T(8,128)(2,1)S(1)}, u32[]{:S(2)}, u32[]{:S(2)}) collective-permute-start(bf16[768,256]{1,0:T(8,128)(2,1)} %param.4), channel_id=1, source_target_pairs={{0,8},{1,9},{2,10},{3,11},{4,12},{5,13},{6,14},{7,15},{8,0},{9,1},... | collective-permute-start | bytes 1179656 | tf_op jit(solution)/shard_map/ppermute | solution.py:15
  29.5 17.6 %collective-permute-start.8 = (bf16[768,256]{1,0:T(8,128)(2,1)S(1)}, bf16[768,256]{1,0:T(8,128)(2,1)S(1)}, u32[]{:S(2)}, u32[]{:S(2)}) collective-permute-start(bf16[768,256]{1,0:T(8,128)(2,1)S(1)} %broadcast_select_fusion), channel_id=1, source_target_pairs={{0,3},{1,4},{2,5},{3,6},{4,7},{5,8},{6,9},{7,10},{8,11},{9,12},{10... | collective-permute-start | bytes 1179656 | tf_op jit(solution)/shard_map/ppermute | solution.py:15
  29.7 5.1 %collective-permute-start.6 = (bf16[768]{0:T(1024)(128)(2,1)S(1)}, bf16[768]{0:T(1024)(128)(2,1)S(1)}, u32[]{:S(2)}, u32[]{:S(2)}) collective-permute-start(bf16[768]{0:T(1024)(128)(2,1)S(1)} %convert_element_type.52), channel_id=1, source_target_pairs={{0,8},{1,9},{2,10},{3,11},{4,12},{5,13},{6,14},{7,15},{8,0},{9,1},... | collective-permute-start | bytes 4616 | tf_op jit(solution)/shard_map/ppermute | solution.py:15
  29.7 17.6 %collective-permute-start.5 = (bf16[768,256]{1,0:T(8,128)(2,1)S(1)}, bf16[768,256]{1,0:T(8,128)(2,1)S(1)}, u32[]{:S(2)}, u32[]{:S(2)}) collective-permute-start(bf16[768,256]{1,0:T(8,128)(2,1)S(1)} %broadcast_select_fusion), channel_id=1, source_target_pairs={{0,4},{1,5},{2,6},{3,7},{4,8},{5,9},{6,10},{7,11},{8,12},{9,13},{1... | collective-permute-start | bytes 1179656 | tf_op jit(solution)/shard_map/ppermute | solution.py:15
  34.7 12.3 %collective-permute-start.9 = (bf16[768]{0:T(1024)(128)(2,1)S(1)}, bf16[768]{0:T(1024)(128)(2,1)S(1)}, u32[]{:S(2)}, u32[]{:S(2)}) collective-permute-start(bf16[768]{0:T(1024)(128)(2,1)S(1)} %broadcast_select_fusion.1), channel_id=1, source_target_pairs={{0,3},{1,4},{2,5},{3,6},{4,7},{5,8},{6,9},{7,10},{8,11},{9,12},{10... | collective-permute-start | bytes 4616 | tf_op jit(solution)/shard_map/ppermute | solution.py:15
  40.4 6.7 %collective-permute-start.7 = (bf16[768]{0:T(1024)(128)(2,1)S(1)}, bf16[768]{0:T(1024)(128)(2,1)S(1)}, u32[]{:S(2)}, u32[]{:S(2)}) collective-permute-start(bf16[768]{0:T(1024)(128)(2,1)S(1)} %broadcast_select_fusion.1), channel_id=1, source_target_pairs={{0,4},{1,5},{2,6},{3,7},{4,8},{5,9},{6,10},{7,11},{8,12},{9,13},{1... | collective-permute-start | bytes 4616 | tf_op jit(solution)/shard_map/ppermute | solution.py:15
  49.4 16.6 %collective-permute-start = (bf16[768,256]{1,0:T(8,128)(2,1)S(1)}, bf16[768,256]{1,0:T(8,128)(2,1)S(1)}, u32[]{:S(2)}, u32[]{:S(2)}) collective-permute-start(bf16[768,256]{1,0:T(8,128)(2,1)S(1)} %get-tuple-element.178), channel_id=1, source_target_pairs={{0,15},{1,0},{2,1},{3,2},{4,3},{5,4},{6,5},{7,6},{8,7},{9,8},{10,9... | collective-permute-start | bytes 1179656 | tf_op jit(solution)/shard_map/while/body/eval_jaxpr/ppermute | solution.py:15
  55.8 10.4 %collective-permute-start.2 = (bf16[768,256]{1,0:T(8,128)(2,1)S(1)}, bf16[768,256]{1,0:T(8,128)(2,1)S(1)}, u32[]{:S(2)}, u32[]{:S(2)}) collective-permute-start(bf16[768,256]{1,0:T(8,128)(2,1)S(1)} %get-tuple-element.176), channel_id=1, source_target_pairs={{0,1},{1,2},{2,3},{3,4},{4,5},{5,6},{6,7},{7,8},{8,9},{9,10},{10,1... | collective-permute-start | bytes 1179656 | tf_op jit(solution)/shard_map/while/body/eval_jaxpr/ppermute | solution.py:15
  55.8 5.7 %collective-permute-start.1 = (bf16[768]{0:T(1024)(128)(2,1)S(1)}, bf16[768]{0:T(1024)(128)(2,1)S(1)}, u32[]{:S(2)}, u32[]{:S(2)}) collective-permute-start(bf16[768]{0:T(1024)(128)(2,1)S(1)} %get-tuple-element.179), channel_id=1, source_target_pairs={{0,15},{1,0},{2,1},{3,2},{4,3},{5,4},{6,5},{7,6},{8,7},{9,8},{10,9... | collective-permute-start | bytes 4616 | tf_op jit(solution)/shard_map/while/body/eval_jaxpr/ppermute | solution.py:15
  60.3 5.7 %collective-permute-start.3 = (bf16[768]{0:T(1024)(128)(2,1)S(1)}, bf16[768]{0:T(1024)(128)(2,1)S(1)}, u32[]{:S(2)}, u32[]{:S(2)}) collective-permute-start(bf16[768]{0:T(1024)(128)(2,1)S(1)} %get-tuple-element.177), channel_id=1, source_target_pairs={{0,1},{1,2},{2,3},{3,4},{4,5},{5,6},{6,7},{7,8},{8,9},{9,10},{10,1... | collective-permute-start | bytes 4616 | tf_op jit(solution)/shard_map/while/body/eval_jaxpr/ppermute | solution.py:15
  70.5 10.3 %collective-permute-start = (bf16[768,256]{1,0:T(8,128)(2,1)S(1)}, bf16[768,256]{1,0:T(8,128)(2,1)S(1)}, u32[]{:S(2)}, u32[]{:S(2)}) collective-permute-start(bf16[768,256]{1,0:T(8,128)(2,1)S(1)} %get-tuple-element.178), channel_id=1, source_target_pairs={{0,15},{1,0},{2,1},{3,2},{4,3},{5,4},{6,5},{7,6},{8,7},{9,8},{10,9... | collective-permute-start | bytes 1179656 | tf_op jit(solution)/shard_map/while/body/eval_jaxpr/ppermute | solution.py:15
  70.6 10.4 %collective-permute-start.2 = (bf16[768,256]{1,0:T(8,128)(2,1)S(1)}, bf16[768,256]{1,0:T(8,128)(2,1)S(1)}, u32[]{:S(2)}, u32[]{:S(2)}) collective-permute-start(bf16[768,256]{1,0:T(8,128)(2,1)S(1)} %get-tuple-element.176), channel_id=1, source_target_pairs={{0,1},{1,2},{2,3},{3,4},{4,5},{5,6},{6,7},{7,8},{8,9},{9,10},{10,1... | collective-permute-start | bytes 1179656 | tf_op jit(solution)/shard_map/while/body/eval_jaxpr/ppermute | solution.py:15
  71.1 5.3 %collective-permute-start.1 = (bf16[768]{0:T(1024)(128)(2,1)S(1)}, bf16[768]{0:T(1024)(128)(2,1)S(1)}, u32[]{:S(2)}, u32[]{:S(2)}) collective-permute-start(bf16[768]{0:T(1024)(128)(2,1)S(1)} %get-tuple-element.179), channel_id=1, source_target_pairs={{0,15},{1,0},{2,1},{3,2},{4,3},{5,4},{6,5},{7,6},{8,7},{9,8},{10,9... | collective-permute-start | bytes 4616 | tf_op jit(solution)/shard_map/while/body/eval_jaxpr/ppermute | solution.py:15
  75.1 5.7 %collective-permute-start.3 = (bf16[768]{0:T(1024)(128)(2,1)S(1)}, bf16[768]{0:T(1024)(128)(2,1)S(1)}, u32[]{:S(2)}, u32[]{:S(2)}) collective-permute-start(bf16[768]{0:T(1024)(128)(2,1)S(1)} %get-tuple-element.177), channel_id=1, source_target_pairs={{0,1},{1,2},{2,3},{3,4},{4,5},{5,6},{6,7},{7,8},{8,9},{9,10},{10,1... | collective-permute-start | bytes 4616 | tf_op jit(solution)/shard_map/while/body/eval_jaxpr/ppermute | solution.py:15
  85.3 10.3 %collective-permute-start = (bf16[768,256]{1,0:T(8,128)(2,1)S(1)}, bf16[768,256]{1,0:T(8,128)(2,1)S(1)}, u32[]{:S(2)}, u32[]{:S(2)}) collective-permute-start(bf16[768,256]{1,0:T(8,128)(2,1)S(1)} %get-tuple-element.178), channel_id=1, source_target_pairs={{0,15},{1,0},{2,1},{3,2},{4,3},{5,4},{6,5},{7,6},{8,7},{9,8},{10,9... | collective-permute-start | bytes 1179656 | tf_op jit(solution)/shard_map/while/body/eval_jaxpr/ppermute | solution.py:15
  85.4 10.4 %collective-permute-start.2 = (bf16[768,256]{1,0:T(8,128)(2,1)S(1)}, bf16[768,256]{1,0:T(8,128)(2,1)S(1)}, u32[]{:S(2)}, u32[]{:S(2)}) collective-permute-start(bf16[768,256]{1,0:T(8,128)(2,1)S(1)} %get-tuple-element.176), channel_id=1, source_target_pairs={{0,1},{1,2},{2,3},{3,4},{4,5},{5,6},{6,7},{7,8},{8,9},{9,10},{10,1... | collective-permute-start | bytes 1179656 | tf_op jit(solution)/shard_map/while/body/eval_jaxpr/ppermute | solution.py:15
  86.9 4.3 %collective-permute-start.1 = (bf16[768]{0:T(1024)(128)(2,1)S(1)}, bf16[768]{0:T(1024)(128)(2,1)S(1)}, u32[]{:S(2)}, u32[]{:S(2)}) collective-permute-start(bf16[768]{0:T(1024)(128)(2,1)S(1)} %get-tuple-element.179), channel_id=1, source_target_pairs={{0,15},{1,0},{2,1},{3,2},{4,3},{5,4},{6,5},{7,6},{8,7},{9,8},{10,9... | collective-permute-start | bytes 4616 | tf_op jit(solution)/shard_map/while/body/eval_jaxpr/ppermute | solution.py:15
  89.9 5.7 %collective-permute-start.3 = (bf16[768]{0:T(1024)(128)(2,1)S(1)}, bf16[768]{0:T(1024)(128)(2,1)S(1)}, u32[]{:S(2)}, u32[]{:S(2)}) collective-permute-start(bf16[768]{0:T(1024)(128)(2,1)S(1)} %get-tuple-element.177), channel_id=1, source_target_pairs={{0,1},{1,2},{2,3},{3,4},{4,5},{5,6},{6,7},{7,8},{8,9},{9,10},{10,1... | collective-permute-start | bytes 4616 | tf_op jit(solution)/shard_map/while/body/eval_jaxpr/ppermute | solution.py:15
  100.2 0.9 copy-start.2
  135.9 34.5 %copy-start = (f32[768,256]{1,0:T(8,128)S(1)}, f32[768,256]{1,0:T(8,128)}, u32[]{:S(2)}) copy-start(f32[768,256]{1,0:T(8,128)} %all-reduce.3.cloned.1.call-done) | copy-start | bytes 2359300
Sparse Core Ops, SparseCore 0:
  101.2 34.6 all-reduce.2
where the time goes:
time: 179 us; the launch traced here: 178 us
  waiting for transfers between devices  72.6 us (41%)
  starting transfers between devices  38.7 us (22%)
  blocking collectives  33 us (18%)
  matrix products  14.1 us (8%)
  between operations  13.5 us (8%)
  other arithmetic  5.07 us (3%)
    ppermute x18, starting transfers between devices, from_behind(): lax.ppermute(x, axis, [(i, (i + by) % devices) for i in range(devices)])  38.7 us
    ppermute x18, waiting for transfers between devices, from_behind(): lax.ppermute(x, axis, [(i, (i + by) % devices) for i in range(devices)])  37.7 us
    psum x1, waiting for transfers between devices, shards(): row_sums = lax.psum(partial_value, 'layer')  34.8 us
    psum x1, blocking collectives, shards(): lax.psum((jnp.sum(member_f * row_sums, axis=0), jnp.sum(member_f, axis=0)...  33 us
    dot_general x8, matrix products, accumulate(): jnp.dot(kernel, onehot, preferred_element_type=jnp.float32)  14.1 us
  transfers between devices with their start and end apart: 19, of which 9 were waited for; matrix products, arithmetic and copies ran while one was open for 1% of the time, Pallas kernels for 0%

commit v1 on v0

--- a/solution.py
+++ b/solution.py
@@ -84,7 +84,7 @@
         split_turn,
         (partial_value, climbing[0], climbing[1], falling[0], falling[1]),
     )[0]
-    row_sums = lax.psum(partial_value, "layer")
+    row_sums = jnp.sum(lax.all_gather(partial_value, "layer"), axis=0)
     member_f = (labels[:, None] == jnp.arange(K, dtype=jnp.int32)[None, :]).astype(jnp.float32)
     within, counts = lax.psum(
         (jnp.sum(member_f * row_sums, axis=0), jnp.sum(member_f, axis=0)), "blk"

time: 179 us -> 172 us (0.961)
  waiting for transfers between devices: 72.6 us -> 63.7 us
  other arithmetic: 5.07 us -> 7.86 us
    psum x1 -> x0, waiting for transfers between devices: 34.8 us -> none  [shards(): row_sums = lax.psum(partial_value, 'layer')]
    all_gather x0 -> x1, waiting for transfers between devices: none -> 27.6 us  [shards(): row_sums = jnp.sum(lax.all_gather(partial_value, 'layer'), axis=0)]
  transfers between devices with their start and end apart: 19 -> 19, of which waited for: 9 -> 9; matrix products, arithmetic and copies ran while one was open for 1% -> 2% of each run, Pallas kernels for 0% -> 0%
where the time goes in v1:
time: 172 us; the launch traced here: 171 us
  waiting for transfers between devices  63.7 us (37%)
  starting transfers between devices  38 us (22%)
  blocking collectives  33 us (19%)
  matrix products  14.1 us (8%)
  between operations  13.5 us (8%)
  other arithmetic  7.86 us (5%)
    ppermute x18, starting transfers between devices, from_behind(): lax.ppermute(x, axis, [(i, (i + by) % devices) for i in range(devices)])  38 us
    ppermute x18, waiting for transfers between devices, from_behind(): lax.ppermute(x, axis, [(i, (i + by) % devices) for i in range(devices)])  36.1 us
    psum x1, blocking collectives, shards(): lax.psum((jnp.sum(member_f * row_sums, axis=0), jnp.sum(member_f, axis=0)...  33 us
    all_gather x1, waiting for transfers between devices, shards(): row_sums = jnp.sum(lax.all_gather(partial_value, 'layer'), axis=0)  27.6 us
    dot_general x8, matrix products, accumulate(): jnp.dot(kernel, onehot, preferred_element_type=jnp.float32)  14.1 us
  transfers between devices with their start and end apart: 19, of which 9 were waited for; matrix products, arithmetic and copies ran while one was open for 2% of the time, Pallas kernels for 0%

profile of v1, /device:TPU:0, one launch (start us, length us, event | category | flops | bytes accessed | tf_op | source)
XLA Modules:
  0.0 171.4 jit_solution(13927080865881720366)
XLA Ops:
  6.5 4.1 %collective-permute-start.4 = (bf16[768,256]{1,0:T(8,128)(2,1)}, bf16[768,256]{1,0:T(8,128)(2,1)S(1)}, u32[]{:S(2)}, u32[]{:S(2)}) collective-permute-start(bf16[768,256]{1,0:T(8,128)(2,1)} %param.4), channel_id=1, source_target_pairs={{0,8},{1,9},{2,10},{3,11},{4,12},{5,13},{6,14},{7,15},{8,0},{9,1},... | collective-permute-start | bytes 1179656 | tf_op jit(solution)/shard_map/ppermute | solution.py:15
  10.6 17.8 %collective-permute-done.4 = bf16[768,256]{1,0:T(8,128)(2,1)S(1)} collective-permute-done((bf16[768,256]{1,0:T(8,128)(2,1)}, bf16[768,256]{1,0:T(8,128)(2,1)S(1)}, u32[]{:S(2)}, u32[]{:S(2)}) %collective-permute-start.4) | collective-permute-done | bytes 393248 | tf_op jit(solution)/shard_map/ppermute | solution.py:15
  28.4 1.0 broadcast_select_fusion
  30.3 5.0 %collective-permute-start.5 = (bf16[768,256]{1,0:T(8,128)(2,1)S(1)}, bf16[768,256]{1,0:T(8,128)(2,1)S(1)}, u32[]{:S(2)}, u32[]{:S(2)}) collective-permute-start(bf16[768,256]{1,0:T(8,128)(2,1)S(1)} %broadcast_select_fusion), channel_id=1, source_target_pairs={{0,4},{1,5},{2,6},{3,7},{4,8},{5,9},{6,10},{7,11},{8,12},{9,13},{1... | collective-permute-start | bytes 1179656 | tf_op jit(solution)/shard_map/ppermute | solution.py:15
  36.1 5.0 %collective-permute-start.9 = (bf16[768]{0:T(1024)(128)(2,1)S(1)}, bf16[768]{0:T(1024)(128)(2,1)S(1)}, u32[]{:S(2)}, u32[]{:S(2)}) collective-permute-start(bf16[768]{0:T(1024)(128)(2,1)S(1)} %broadcast_select_fusion.1), channel_id=1, source_target_pairs={{0,3},{1,4},{2,5},{3,6},{4,7},{5,8},{6,9},{7,10},{8,11},{9,12},{10... | collective-permute-start | bytes 4616 | tf_op jit(solution)/shard_map/ppermute | solution.py:15
  41.0 3.7 %collective-permute-start.7 = (bf16[768]{0:T(1024)(128)(2,1)S(1)}, bf16[768]{0:T(1024)(128)(2,1)S(1)}, u32[]{:S(2)}, u32[]{:S(2)}) collective-permute-start(bf16[768]{0:T(1024)(128)(2,1)S(1)} %broadcast_select_fusion.1), channel_id=1, source_target_pairs={{0,4},{1,5},{2,6},{3,7},{4,8},{5,9},{6,10},{7,11},{8,12},{9,13},{1... | collective-permute-start | bytes 4616 | tf_op jit(solution)/shard_map/ppermute | solution.py:15
  44.8 1.2 multiply_reduce_fusion.4
  46.0 1.1 collective-permute-done.9
  47.5 0.9 fusion.29
  48.4 0.9 fusion.30
  49.4 50.8 %while.20 = (s32[]{:T(128)}, f32[768,256]{1,0:T(8,128)S(1)}, bf16[768,256]{1,0:T(8,128)(2,1)S(1)}, bf16[768]{0:T(1024)(128)(2,1)S(1)}, bf16[768,256]{1,0:T(8,128...) while((s32[]{:T(128)}, f32[768,256]{1,0:T(8,128)S(1)}, ...), condition=%wide.region_6.7_spmd.clone.clone, body=%wide.region_3.6_spmd.clone.clone.sunk | while | flops 1217003520 | bytes 10276093 | solution.py:81
  49.4 6.5 %collective-permute-start = (bf16[768,256]{1,0:T(8,128)(2,1)S(1)}, bf16[768,256]{1,0:T(8,128)(2,1)S(1)}, u32[]{:S(2)}, u32[]{:S(2)}) collective-permute-start(bf16[768,256]{1,0:T(8,128)(2,1)S(1)} %get-tuple-element.178), channel_id=1, source_target_pairs={{0,15},{1,0},{2,1},{3,2},{4,3},{5,4},{6,5},{7,6},{8,7},{9,8},{10,9... | collective-permute-start | bytes 1179656 | tf_op jit(solution)/shard_map/while/body/eval_jaxpr/ppermute | solution.py:15
  55.8 4.4 %collective-permute-start.1 = (bf16[768]{0:T(1024)(128)(2,1)S(1)}, bf16[768]{0:T(1024)(128)(2,1)S(1)}, u32[]{:S(2)}, u32[]{:S(2)}) collective-permute-start(bf16[768]{0:T(1024)(128)(2,1)S(1)} %get-tuple-element.179), channel_id=1, source_target_pairs={{0,15},{1,0},{2,1},{3,2},{4,3},{5,4},{6,5},{7,6},{8,7},{9,8},{10,9... | collective-permute-start | bytes 4616 | tf_op jit(solution)/shard_map/while/body/eval_jaxpr/ppermute | solution.py:15
  60.3 1.3 collective-permute-done.1
  61.6 4.4 %collective-permute-done.3 = bf16[768]{0:T(1024)(128)(2,1)S(1)} collective-permute-done((bf16[768]{0:T(1024)(128)(2,1)S(1)}, bf16[768]{0:T(1024)(128)(2,1)S(1)}, u32[]{:S(2)}, u32[]{:S(2)}) %collective-permute-start.3) | collective-permute-done | bytes 1568 | tf_op jit(solution)/shard_map/while/body/eval_jaxpr/ppermute | solution.py:15
  66.4 1.8 %fusion.63 = f32[768,256]{1,0:T(8,128)} fusion(bf16[768,256]{1,0:T(8,128)(2,1)S(1)} %get-tuple-element.190, bf16[768,256]{1,0:T(8,128)(2,1)S(1)} %collective-permute-done, f32[768]{0:T(1024)S(1)} %multiply_reduce_fusion.7, f32[768]{0:T(1024)S(1)} %get-tuple-element.189, f32[768]{0:T(1024)S(1)} %convert_element_type.105), kind=kOutput, calls=%fused_computation.4.clone.1 | convolution fusion | flops 607715328 | bytes 1582080 | tf_op jit(solution)/shard_map/while/body/eval_jaxpr/dot_general | solution.py:48
  68.3 2.2 %fusion.64 = f32[768,256]{1,0:T(8,128)S(1)} fusion(f32[768,256]{1,0:T(8,128)} %fusion.63, f32[768,256]{1,0:T(8,128)S(1)} %get-tuple-element.175, bf16[768,256]{1,0:T(8,128)(2,1)S(1)} %get-tuple-element.190, bf16[768,256]{1,0:T(8,128)(2,1)S(1)} %collective-permute-done.2, f32[768]{0:T(1024)S(1)} %multiply_reduce_fusion.8, ...), kind=kOutput, calls=%fused_computation.6.clone.1 | convolution fusion | flops 608108544 | bytes 3154944 | tf_op jit(solution)/shard_map/while/body/eval_jaxpr/dot_general | solution.py:48
  71.1 4.0 %collective-permute-start.1 = (bf16[768]{0:T(1024)(128)(2,1)S(1)}, bf16[768]{0:T(1024)(128)(2,1)S(1)}, u32[]{:S(2)}, u32[]{:S(2)}) collective-permute-start(bf16[768]{0:T(1024)(128)(2,1)S(1)} %get-tuple-element.179), channel_id=1, source_target_pairs={{0,15},{1,0},{2,1},{3,2},{4,3},{5,4},{6,5},{7,6},{8,7},{9,8},{10,9... | collective-permute-start | bytes 4616 | tf_op jit(solution)/shard_map/while/body/eval_jaxpr/ppermute | solution.py:15
  75.1 1.3 collective-permute-done.1
  76.4 4.4 %collective-permute-done.3 = bf16[768]{0:T(1024)(128)(2,1)S(1)} collective-permute-done((bf16[768]{0:T(1024)(128)(2,1)S(1)}, bf16[768]{0:T(1024)(128)(2,1)S(1)}, u32[]{:S(2)}, u32[]{:S(2)}) %collective-permute-start.3) | collective-permute-done | bytes 1568 | tf_op jit(solution)/shard_map/while/body/eval_jaxpr/ppermute | solution.py:15
  81.3 1.8 %fusion.63 = f32[768,256]{1,0:T(8,128)} fusion(bf16[768,256]{1,0:T(8,128)(2,1)S(1)} %get-tuple-element.190, bf16[768,256]{1,0:T(8,128)(2,1)S(1)} %collective-permute-done, f32[768]{0:T(1024)S(1)} %multiply_reduce_fusion.7, f32[768]{0:T(1024)S(1)} %get-tuple-element.189, f32[768]{0:T(1024)S(1)} %convert_element_type.105), kind=kOutput, calls=%fused_computation.4.clone.1 | convolution fusion | flops 607715328 | bytes 1582080 | tf_op jit(solution)/shard_map/while/body/eval_jaxpr/dot_general | solution.py:48
  83.1 2.2 %fusion.64 = f32[768,256]{1,0:T(8,128)S(1)} fusion(f32[768,256]{1,0:T(8,128)} %fusion.63, f32[768,256]{1,0:T(8,128)S(1)} %get-tuple-element.175, bf16[768,256]{1,0:T(8,128)(2,1)S(1)} %get-tuple-element.190, bf16[768,256]{1,0:T(8,128)(2,1)S(1)} %collective-permute-done.2, f32[768]{0:T(1024)S(1)} %multiply_reduce_fusion.8, ...), kind=kOutput, calls=%fused_computation.6.clone.1 | convolution fusion | flops 608108544 | bytes 3154944 | tf_op jit(solution)/shard_map/while/body/eval_jaxpr/dot_general | solution.py:48
  85.4 1.4 collective-permute-start.2
  86.9 3.0 %collective-permute-start.1 = (bf16[768]{0:T(1024)(128)(2,1)S(1)}, bf16[768]{0:T(1024)(128)(2,1)S(1)}, u32[]{:S(2)}, u32[]{:S(2)}) collective-permute-start(bf16[768]{0:T(1024)(128)(2,1)S(1)} %get-tuple-element.179), channel_id=1, source_target_pairs={{0,15},{1,0},{2,1},{3,2},{4,3},{5,4},{6,5},{7,6},{8,7},{9,8},{10,9... | collective-permute-start | bytes 4616 | tf_op jit(solution)/shard_map/while/body/eval_jaxpr/ppermute | solution.py:15
  89.9 1.3 collective-permute-done.1
  91.2 4.4 %collective-permute-done.3 = bf16[768]{0:T(1024)(128)(2,1)S(1)} collective-permute-done((bf16[768]{0:T(1024)(128)(2,1)S(1)}, bf16[768]{0:T(1024)(128)(2,1)S(1)}, u32[]{:S(2)}, u32[]{:S(2)}) %collective-permute-start.3) | collective-permute-done | bytes 1568 | tf_op jit(solution)/shard_map/while/body/eval_jaxpr/ppermute | solution.py:15
  96.1 1.8 %fusion.63 = f32[768,256]{1,0:T(8,128)} fusion(bf16[768,256]{1,0:T(8,128)(2,1)S(1)} %get-tuple-element.190, bf16[768,256]{1,0:T(8,128)(2,1)S(1)} %collective-permute-done, f32[768]{0:T(1024)S(1)} %multiply_reduce_fusion.7, f32[768]{0:T(1024)S(1)} %get-tuple-element.189, f32[768]{0:T(1024)S(1)} %convert_element_type.105), kind=kOutput, calls=%fused_computation.4.clone.1 | convolution fusion | flops 607715328 | bytes 1582080 | tf_op jit(solution)/shard_map/while/body/eval_jaxpr/dot_general | solution.py:48
  97.9 2.2 %fusion.64 = f32[768,256]{1,0:T(8,128)S(1)} fusion(f32[768,256]{1,0:T(8,128)} %fusion.63, f32[768,256]{1,0:T(8,128)S(1)} %get-tuple-element.175, bf16[768,256]{1,0:T(8,128)(2,1)S(1)} %get-tuple-element.190, bf16[768,256]{1,0:T(8,128)(2,1)S(1)} %collective-permute-done.2, f32[768]{0:T(1024)S(1)} %multiply_reduce_fusion.8, ...), kind=kOutput, calls=%fused_computation.6.clone.1 | convolution fusion | flops 608108544 | bytes 3154944 | tf_op jit(solution)/shard_map/while/body/eval_jaxpr/dot_general | solution.py:48
  101.1 27.6 %all-gather.3.cloned.1.call-done = f32[1536,256]{1,0:T(8,128)} async-done(((f32[768,256]{1,0:T(8,128)}), f32[1536,256]{1,0:T(8,128)}) %all-gather.3.cloned.1.call-update) | async-done | bytes 1572880 | tf_op jit(solution)/shard_map/all_gather | solution.py:87
  128.7 1.6 reduce_sum.75
  130.5 33.0 %all-reduce = (f32[256]{0:T(256)S(1)}, f32[256]{0:T(256)S(1)}) all-reduce(f32[256]{0:T(256)S(1)} %get-tuple-element.97, f32[256]{0:T(256)S(1)} %get-tuple-element.96), channel_id=1, replica_groups=mesh['layer'=2,'blk'=16] {'blk'}, use_global_device_ids=true, to_apply=%region_11.12 | all-reduce | flops 512 | bytes 4096 | tf_op jit(solution)/shard_map/psum | solution.py:89
  163.6 1.0 subtract_add_fusion
  (59 shorter events, 5.0 us)
Async XLA Ops:
  6.5 40.9 %copy-start = (bf16[768,256]{1,0:T(8,128)(2,1)S(1)}, bf16[768,256]{1,0:T(8,128)(2,1)}, u32[]{:S(2)}) copy-start(bf16[768,256]{1,0:T(8,128)(2,1)} %param.4) | copy-start | bytes 1179652
  6.5 122.2 %all-gather.3.cloned.1.call-start = ((), (), s32[]{:S(2)}) async-start(), calls=%async_computation | async-start | bytes 2359296 | tf_op jit(solution)/shard_map/all_gather | solution.py:87
  6.5 21.9 %collective-permute-start.4 = (bf16[768,256]{1,0:T(8,128)(2,1)}, bf16[768,256]{1,0:T(8,128)(2,1)S(1)}, u32[]{:S(2)}, u32[]{:S(2)}) collective-permute-start(bf16[768,256]{1,0:T(8,128)(2,1)} %param.4), channel_id=1, source_target_pairs={{0,8},{1,9},{2,10},{3,11},{4,12},{5,13},{6,14},{7,15},{8,0},{9,1},... | collective-permute-start | bytes 1179656 | tf_op jit(solution)/shard_map/ppermute | solution.py:15
  29.5 17.6 %collective-permute-start.8 = (bf16[768,256]{1,0:T(8,128)(2,1)S(1)}, bf16[768,256]{1,0:T(8,128)(2,1)S(1)}, u32[]{:S(2)}, u32[]{:S(2)}) collective-permute-start(bf16[768,256]{1,0:T(8,128)(2,1)S(1)} %broadcast_select_fusion), channel_id=1, source_target_pairs={{0,3},{1,4},{2,5},{3,6},{4,7},{5,8},{6,9},{7,10},{8,11},{9,12},{10... | collective-permute-start | bytes 1179656 | tf_op jit(solution)/shard_map/ppermute | solution.py:15
  30.3 5.1 %collective-permute-start.6 = (bf16[768]{0:T(1024)(128)(2,1)S(1)}, bf16[768]{0:T(1024)(128)(2,1)S(1)}, u32[]{:S(2)}, u32[]{:S(2)}) collective-permute-start(bf16[768]{0:T(1024)(128)(2,1)S(1)} %convert_element_type.52), channel_id=1, source_target_pairs={{0,8},{1,9},{2,10},{3,11},{4,12},{5,13},{6,14},{7,15},{8,0},{9,1},... | collective-permute-start | bytes 4616 | tf_op jit(solution)/shard_map/ppermute | solution.py:15
  30.3 16.9 %collective-permute-start.5 = (bf16[768,256]{1,0:T(8,128)(2,1)S(1)}, bf16[768,256]{1,0:T(8,128)(2,1)S(1)}, u32[]{:S(2)}, u32[]{:S(2)}) collective-permute-start(bf16[768,256]{1,0:T(8,128)(2,1)S(1)} %broadcast_select_fusion), channel_id=1, source_target_pairs={{0,4},{1,5},{2,6},{3,7},{4,8},{5,9},{6,10},{7,11},{8,12},{9,13},{1... | collective-permute-start | bytes 1179656 | tf_op jit(solution)/shard_map/ppermute | solution.py:15
  36.1 11.0 %collective-permute-start.9 = (bf16[768]{0:T(1024)(128)(2,1)S(1)}, bf16[768]{0:T(1024)(128)(2,1)S(1)}, u32[]{:S(2)}, u32[]{:S(2)}) collective-permute-start(bf16[768]{0:T(1024)(128)(2,1)S(1)} %broadcast_select_fusion.1), channel_id=1, source_target_pairs={{0,3},{1,4},{2,5},{3,6},{4,7},{5,8},{6,9},{7,10},{8,11},{9,12},{10... | collective-permute-start | bytes 4616 | tf_op jit(solution)/shard_map/ppermute | solution.py:15
  41.0 6.0 %collective-permute-start.7 = (bf16[768]{0:T(1024)(128)(2,1)S(1)}, bf16[768]{0:T(1024)(128)(2,1)S(1)}, u32[]{:S(2)}, u32[]{:S(2)}) collective-permute-start(bf16[768]{0:T(1024)(128)(2,1)S(1)} %broadcast_select_fusion.1), channel_id=1, source_target_pairs={{0,4},{1,5},{2,6},{3,7},{4,8},{5,9},{6,10},{7,11},{8,12},{9,13},{1... | collective-permute-start | bytes 4616 | tf_op jit(solution)/shard_map/ppermute | solution.py:15
  49.4 16.6 %collective-permute-start = (bf16[768,256]{1,0:T(8,128)(2,1)S(1)}, bf16[768,256]{1,0:T(8,128)(2,1)S(1)}, u32[]{:S(2)}, u32[]{:S(2)}) collective-permute-start(bf16[768,256]{1,0:T(8,128)(2,1)S(1)} %get-tuple-element.178), channel_id=1, source_target_pairs={{0,15},{1,0},{2,1},{3,2},{4,3},{5,4},{6,5},{7,6},{8,7},{9,8},{10,9... | collective-permute-start | bytes 1179656 | tf_op jit(solution)/shard_map/while/body/eval_jaxpr/ppermute | solution.py:15
  55.8 10.4 %collective-permute-start.2 = (bf16[768,256]{1,0:T(8,128)(2,1)S(1)}, bf16[768,256]{1,0:T(8,128)(2,1)S(1)}, u32[]{:S(2)}, u32[]{:S(2)}) collective-permute-start(bf16[768,256]{1,0:T(8,128)(2,1)S(1)} %get-tuple-element.176), channel_id=1, source_target_pairs={{0,1},{1,2},{2,3},{3,4},{4,5},{5,6},{6,7},{7,8},{8,9},{9,10},{10,1... | collective-permute-start | bytes 1179656 | tf_op jit(solution)/shard_map/while/body/eval_jaxpr/ppermute | solution.py:15
  55.8 5.7 %collective-permute-start.1 = (bf16[768]{0:T(1024)(128)(2,1)S(1)}, bf16[768]{0:T(1024)(128)(2,1)S(1)}, u32[]{:S(2)}, u32[]{:S(2)}) collective-permute-start(bf16[768]{0:T(1024)(128)(2,1)S(1)} %get-tuple-element.179), channel_id=1, source_target_pairs={{0,15},{1,0},{2,1},{3,2},{4,3},{5,4},{6,5},{7,6},{8,7},{9,8},{10,9... | collective-permute-start | bytes 4616 | tf_op jit(solution)/shard_map/while/body/eval_jaxpr/ppermute | solution.py:15
  60.3 5.7 %collective-permute-start.3 = (bf16[768]{0:T(1024)(128)(2,1)S(1)}, bf16[768]{0:T(1024)(128)(2,1)S(1)}, u32[]{:S(2)}, u32[]{:S(2)}) collective-permute-start(bf16[768]{0:T(1024)(128)(2,1)S(1)} %get-tuple-element.177), channel_id=1, source_target_pairs={{0,1},{1,2},{2,3},{3,4},{4,5},{5,6},{6,7},{7,8},{8,9},{9,10},{10,1... | collective-permute-start | bytes 4616 | tf_op jit(solution)/shard_map/while/body/eval_jaxpr/ppermute | solution.py:15
  70.5 10.3 %collective-permute-start = (bf16[768,256]{1,0:T(8,128)(2,1)S(1)}, bf16[768,256]{1,0:T(8,128)(2,1)S(1)}, u32[]{:S(2)}, u32[]{:S(2)}) collective-permute-start(bf16[768,256]{1,0:T(8,128)(2,1)S(1)} %get-tuple-element.178), channel_id=1, source_target_pairs={{0,15},{1,0},{2,1},{3,2},{4,3},{5,4},{6,5},{7,6},{8,7},{9,8},{10,9... | collective-permute-start | bytes 1179656 | tf_op jit(solution)/shard_map/while/body/eval_jaxpr/ppermute | solution.py:15
  70.6 10.4 %collective-permute-start.2 = (bf16[768,256]{1,0:T(8,128)(2,1)S(1)}, bf16[768,256]{1,0:T(8,128)(2,1)S(1)}, u32[]{:S(2)}, u32[]{:S(2)}) collective-permute-start(bf16[768,256]{1,0:T(8,128)(2,1)S(1)} %get-tuple-element.176), channel_id=1, source_target_pairs={{0,1},{1,2},{2,3},{3,4},{4,5},{5,6},{6,7},{7,8},{8,9},{9,10},{10,1... | collective-permute-start | bytes 1179656 | tf_op jit(solution)/shard_map/while/body/eval_jaxpr/ppermute | solution.py:15
  71.1 5.3 %collective-permute-start.1 = (bf16[768]{0:T(1024)(128)(2,1)S(1)}, bf16[768]{0:T(1024)(128)(2,1)S(1)}, u32[]{:S(2)}, u32[]{:S(2)}) collective-permute-start(bf16[768]{0:T(1024)(128)(2,1)S(1)} %get-tuple-element.179), channel_id=1, source_target_pairs={{0,15},{1,0},{2,1},{3,2},{4,3},{5,4},{6,5},{7,6},{8,7},{9,8},{10,9... | collective-permute-start | bytes 4616 | tf_op jit(solution)/shard_map/while/body/eval_jaxpr/ppermute | solution.py:15
  75.1 5.7 %collective-permute-start.3 = (bf16[768]{0:T(1024)(128)(2,1)S(1)}, bf16[768]{0:T(1024)(128)(2,1)S(1)}, u32[]{:S(2)}, u32[]{:S(2)}) collective-permute-start(bf16[768]{0:T(1024)(128)(2,1)S(1)} %get-tuple-element.177), channel_id=1, source_target_pairs={{0,1},{1,2},{2,3},{3,4},{4,5},{5,6},{6,7},{7,8},{8,9},{9,10},{10,1... | collective-permute-start | bytes 4616 | tf_op jit(solution)/shard_map/while/body/eval_jaxpr/ppermute | solution.py:15
  85.3 10.3 %collective-permute-start = (bf16[768,256]{1,0:T(8,128)(2,1)S(1)}, bf16[768,256]{1,0:T(8,128)(2,1)S(1)}, u32[]{:S(2)}, u32[]{:S(2)}) collective-permute-start(bf16[768,256]{1,0:T(8,128)(2,1)S(1)} %get-tuple-element.178), channel_id=1, source_target_pairs={{0,15},{1,0},{2,1},{3,2},{4,3},{5,4},{6,5},{7,6},{8,7},{9,8},{10,9... | collective-permute-start | bytes 1179656 | tf_op jit(solution)/shard_map/while/body/eval_jaxpr/ppermute | solution.py:15
  85.4 10.4 %collective-permute-start.2 = (bf16[768,256]{1,0:T(8,128)(2,1)S(1)}, bf16[768,256]{1,0:T(8,128)(2,1)S(1)}, u32[]{:S(2)}, u32[]{:S(2)}) collective-permute-start(bf16[768,256]{1,0:T(8,128)(2,1)S(1)} %get-tuple-element.176), channel_id=1, source_target_pairs={{0,1},{1,2},{2,3},{3,4},{4,5},{5,6},{6,7},{7,8},{8,9},{9,10},{10,1... | collective-permute-start | bytes 1179656 | tf_op jit(solution)/shard_map/while/body/eval_jaxpr/ppermute | solution.py:15
  86.9 4.3 %collective-permute-start.1 = (bf16[768]{0:T(1024)(128)(2,1)S(1)}, bf16[768]{0:T(1024)(128)(2,1)S(1)}, u32[]{:S(2)}, u32[]{:S(2)}) collective-permute-start(bf16[768]{0:T(1024)(128)(2,1)S(1)} %get-tuple-element.179), channel_id=1, source_target_pairs={{0,15},{1,0},{2,1},{3,2},{4,3},{5,4},{6,5},{7,6},{8,7},{9,8},{10,9... | collective-permute-start | bytes 4616 | tf_op jit(solution)/shard_map/while/body/eval_jaxpr/ppermute | solution.py:15
  89.9 5.7 %collective-permute-start.3 = (bf16[768]{0:T(1024)(128)(2,1)S(1)}, bf16[768]{0:T(1024)(128)(2,1)S(1)}, u32[]{:S(2)}, u32[]{:S(2)}) collective-permute-start(bf16[768]{0:T(1024)(128)(2,1)S(1)} %get-tuple-element.177), channel_id=1, source_target_pairs={{0,1},{1,2},{2,3},{3,4},{4,5},{5,6},{6,7},{7,8},{8,9},{9,10},{10,1... | collective-permute-start | bytes 4616 | tf_op jit(solution)/shard_map/while/body/eval_jaxpr/ppermute | solution.py:15
  100.1 0.9 copy-start.1
  100.2 30.2 %copy-start.2 = (s32[768]{0:T(1024)S(1)}, s32[768]{0:T(1024)}, u32[]{:S(2)}) copy-start(s32[768]{0:T(1024)} %param.5) | copy-start | bytes 9220
Sparse Core Ops, SparseCore 0:
  101.2 27.4 all-gather.2
